TPU v7x, 512 devices: a whole 4x8x8 slice. The times are simulated.
512 devices in a mesh: owner: 32 (over y, x), rows: 16 (over z, core).
Axes of the slice: x: 4, y: 8, z: 8, core: 2. Of those that a mesh axis runs over, the one named last changes fastest.
Arguments:
- w_down: float32 [64, 1408, 2048], P('owner', None, 'rows'), may hold values from -0.21875 to 0.21875
- router_weight: float32 [2048, 64], P('rows', 'owner'), may hold values from -0.125 to 0.125
- router_gain: float32 [2048], P('rows'), may hold values from 0.25 to 1.75
Outputs:
- serve_down: bfloat16 [64, 1408, 2048], P('owner')
- scale_down: float32 [64, 1408], P('owner')
- serve_router: bfloat16 [2048, 64], replicated
All inputs are finite; a program needn't handle non-finite values. Where the computation divides by a largest or mean magnitude, that divisor is 1e-20 or more.
Results may differ from a plain program's by a relative error of at most 0.001.
Values may be sent and summed in bfloat16 or wider, within the bound.
A program may use at most 128 MiB of HBM per device.

v0:
```python
import jax
import jax.numpy as jnp
from jax import lax
from jax.sharding import PartitionSpec as P


def sent_to_all(x, axis):
    copies = jnp.broadcast_to(x, (lax.axis_size(axis), *x.shape))
    return lax.all_to_all(copies, axis, split_axis=0, concat_axis=0, tiled=True)


def of_everyone(x, axis):
    everything = sent_to_all(x, axis)
    return jnp.max(everything, axis=0)


def laid_out(pieces, dim):
    pieces = jnp.moveaxis(pieces, 0, dim)
    lengths = pieces.shape
    return pieces.reshape(*lengths[:dim], lengths[dim] * lengths[dim + 1], *lengths[dim + 2 :])


def collect(x, axis, dim):
    return laid_out(sent_to_all(x, axis), dim)


def on_device(w_down, router_weight, router_gain):
    scale_down = of_everyone(jnp.max(jnp.abs(w_down), axis=2), "rows")
    narrow_down = (w_down / jnp.expand_dims(scale_down, 2)).astype(jnp.bfloat16)
    serve_down = lax.all_gather(narrow_down, "rows", axis=2, tiled=True)
    part_router = (router_weight * router_gain[:, None]).astype(jnp.bfloat16)
    row_router = lax.all_gather(part_router, "rows", axis=0, tiled=True)
    serve_router = collect(row_router, "owner", 1)
    return (serve_down, scale_down, serve_router)


def solution(mesh):
    placed = (P("owner", None, "rows"), P("rows", "owner"), P("rows"))
    return jax.shard_map(
        on_device,
        mesh=mesh,
        in_specs=placed,
        out_specs=(P("owner", None, None), P("owner", None), P()),
        check_vma=False,
    )
```

profile of v0, /device:TPU:1, one launch (start us, length us, event | category | flops | bytes accessed | tf_op | source)
XLA Modules:
  0.0 126.5 jit_solution(15650277266331991324)
XLA Ops:
  7.2 0.0 copy-start
  7.2 0.0 all-gather.2.cloned.1.call-start
  7.2 1.9 %abs_reduce_fusion = f32[2,1408]{1,0:T(2,128)S(1)} fusion(f32[2,1408,128]{2,1,0:T(8,128)} %param.3), kind=kLoop, calls=%fused_computation.1 | loop fusion | flops 718080 | bytes 1453056 | tf_op jit(solution)/shard_map/reduce_max | solution.py:28
  9.2 21.2 %all_to_all.10 = f32[16,2,1408]{2,1,0:T(2,128)S(1)} all-to-all(f32[16,2,1408]{2,1,0:T(2,128)S(1)} %broadcast_in_dim.8), channel_id=1, replica_groups=mesh['owner'=32,'rows'=16] {'rows'}, dimensions={0} | all-to-all | bytes 360448 | tf_op jit(solution)/shard_map/all_to_all | solution.py:9
  30.4 0.1 reduce_max.19
  30.5 0.0 copy-done
  30.5 0.0 copy-start.1
  30.5 0.0 copy-start.2
  30.5 0.0 copy-start.3
  30.5 1.3 %divide_convert_fusion = bf16[2,1408,128]{2,1,0:T(8,128)(2,1)} fusion(f32[2,1408,128]{2,1,0:T(8,128)S(1)} %copy-done, f32[2,1408]{1,0:T(2,128)S(1)} %reduce_max.19), kind=kLoop, calls=%fused_computation | loop fusion | flops 720896 | bytes 2173952 | tf_op jit(solution)/shard_map/convert_element_type | solution.py:29
  31.8 0.0 all-gather.2.cloned.1.call-update
  31.9 0.0 copy-done.1
  31.9 0.0 copy-done.2
  31.9 0.0 copy-done.3
  31.9 14.6 %all_gather.7 = bf16[2048,2]{0,1:T(2,128)(2,1)S(1)} all-gather(bf16[128,2]{0,1:T(2,128)(2,1)S(1)} %multiply_convert_fusion), channel_id=1, replica_groups=mesh['owner'=32,'rows'=16] {'rows'}, dimensions={0}, use_global_device_ids=true | all-gather | bytes 8704 | tf_op jit(solution)/shard_map/all_gather | solution.py:32
  46.5 0.1 broadcast_in_dim.9
  46.7 21.1 %all_to_all.11 = bf16[32,2048,2]{1,2,0:T(2,128)(2,1)S(1)} all-to-all(bf16[32,2048,2]{1,2,0:T(2,128)(2,1)S(1)} %broadcast_in_dim.9), channel_id=1, replica_groups=mesh['owner'=32,'rows'=16] {'owner'}, dimensions={0} | all-to-all | bytes 524288 | tf_op jit(solution)/shard_map/all_to_all | solution.py:9
  67.8 0.8 reshape.11
  68.6 40.9 %all-gather.2.cloned.1.call-done = bf16[2,1408,2048]{2,1,0:T(8,128)(2,1)} async-done(((bf16[2,1408,128]{2,1,0:T(8,128)(2,1)}), bf16[2,1408,2048]{2,1,0:T(8,128)(2,1)}) %all-gather.2.cloned.1.call-update) | async-done | bytes 11534352 | tf_op jit(solution)/shard_map/all_gather | solution.py:30
  109.5 10.1 %copy.9 = bf16[2,1408,2048]{2,1,0:T(8,128)(2,1)} copy(bf16[2,1408,2048]{2,1,0:T(8,128)(2,1)} %all-gather.2.cloned.1.call-done) | data formatting | bytes 23068672
  (2 shorter events, 0.1 us)
Async XLA Ops:
  7.2 23.3 %copy-start = (f32[2,1408,128]{2,1,0:T(8,128)S(1)}, f32[2,1408,128]{2,1,0:T(8,128)}, u32[]{:S(2)}) copy-start(f32[2,1408,128]{2,1,0:T(8,128)} %param.3) | copy-start | bytes 4325380
  7.2 102.4 %all-gather.2.cloned.1.call-start = ((), (), s32[]{:S(2)}) async-start(), calls=%async_computation.2 | async-start | bytes 12255232 | tf_op jit(solution)/shard_map/all_gather | solution.py:30
  30.5 1.4 %copy-start.1 = (f32[2,1408]{1,0:T(2,128)}, f32[2,1408]{1,0:T(2,128)S(1)}, u32[]{:S(2)}) copy-start(f32[2,1408]{1,0:T(2,128)S(1)} %reduce_max.19) | copy-start | bytes 33796
  30.5 1.4 %copy-start.2 = (f32[128,2]{0,1:T(2,128)S(1)}, f32[128,2]{0,1:T(2,128)}, u32[]{:S(2)}) copy-start(f32[128,2]{0,1:T(2,128)} %param.4) | copy-start | bytes 3076
  30.5 1.4 %copy-start.3 = (f32[128]{0:T(128)S(1)}, f32[128]{0:T(128)}, u32[]{:S(2)}) copy-start(f32[128]{0:T(128)} %param.5) | copy-start | bytes 1540
Sparse Core Ops, SparseCore 0:
  32.0 77.4 all-gather.1
where the time goes:
time: 127 us; the launch traced here: 126 us
  blocking collectives  57 us (45%)
  waiting for transfers between devices  41 us (32%)
  between operations  14.1 us (11%)
  local copies, waits for them, and re-layouts  11.1 us (9%)
  other arithmetic  3.29 us (3%)
    all_to_all x2, blocking collectives, sent_to_all(): return lax.all_to_all(copies, axis, split_axis=0, concat_axis=0, tiled=True)  42.3 us
    all_gather x1, waiting for transfers between devices, on_device(): serve_down = lax.all_gather(narrow_down, 'rows', axis=2, tiled=True)  40.9 us
    all_gather x1, blocking collectives, on_device(): row_router = lax.all_gather(part_router, 'rows', axis=0, tiled=True)  14.6 us
    unnamed x9, local copies, waits for them, and re-layouts  10.1 us
  transfers between devices with their start and end apart: 1, of which 1 were waited for; matrix products, arithmetic and copies ran while one was open for 1% of the time, Pallas kernels for 0%

commit v1 on v0

--- a/solution.py
+++ b/solution.py
@@ -27,7 +27,9 @@
 def on_device(w_down, router_weight, router_gain):
     scale_down = of_everyone(jnp.max(jnp.abs(w_down), axis=2), "rows")
     narrow_down = (w_down / jnp.expand_dims(scale_down, 2)).astype(jnp.bfloat16)
-    serve_down = lax.all_gather(narrow_down, "rows", axis=2, tiled=True)
+    serve_down = jnp.concatenate(
+        lax.all_to_all(jnp.stack([narrow_down] * lax.axis_size("rows")), "rows", 0, 0), axis=2
+    )
     part_router = (router_weight * router_gain[:, None]).astype(jnp.bfloat16)
     row_router = lax.all_gather(part_router, "rows", axis=0, tiled=True)
     serve_router = collect(row_router, "owner", 1)

time: 127 us -> 353 us (2.78)
  waiting for transfers between devices: 41 us -> 261 us
  blocking collectives: 57 us -> 18 us
  starting transfers between devices: 0.04 us -> 29.8 us
  local copies, waits for them, and re-layouts: 11.1 us -> 39.8 us
  between operations: 14.1 us -> 0.71 us
    all_to_all x0 -> x3, waiting for transfers between devices: none -> 261 us  [the longest x1 250 us: on_device(): lax.all_to_all(jnp.stack([narrow_down] * lax.axis_size('rows')), 'rows',...]
    all_to_all x2 -> x0, blocking collectives: 42.3 us -> none  [sent_to_all(): return lax.all_to_all(copies, axis, split_axis=0, concat_axis=0, tiled=True)]
    all_gather x1 -> x0, waiting for transfers between devices: 40.9 us -> none  [on_device(): serve_down = lax.all_gather(narrow_down, 'rows', axis=2, tiled=True)]
    all_to_all x0 -> x3, starting transfers between devices: none -> 29.8 us  [the longest x2 21.5 us: sent_to_all(): return lax.all_to_all(copies, axis, split_axis=0, concat_axis=0, tiled=True)]
    all_to_all x0 -> x1, local copies, waits for them, and re-layouts: none -> 15.2 us  [on_device(): lax.all_to_all(jnp.stack([narrow_down] * lax.axis_size('rows')), 'rows',...]
    another operation x0 -> x1, local copies, waits for them, and re-layouts: none -> 7.03 us  [on_device(): jnp.stack([narrow_down] * lax.axis_size('rows'))]
    unnamed x9, local copies, waits for them, and re-layouts: 10.1 us -> 15.3 us
  transfers between devices with their start and end apart: 1 -> 3, of which waited for: 1 -> 2; matrix products, arithmetic and copies ran while one was open for 1% -> 0% of each run, Pallas kernels for 0% -> 0%
where the time goes in v1:
time: 353 us; the launch traced here: 352 us
  waiting for transfers between devices  261 us (74%)
  local copies, waits for them, and re-layouts  39.8 us (11%)
  starting transfers between devices  29.8 us (8%)
  blocking collectives  18 us (5%)
    all_to_all x1, waiting for transfers between devices, on_device(): lax.all_to_all(jnp.stack([narrow_down] * lax.axis_size('rows')), 'rows',...  250 us
    all_to_all x2, starting transfers between devices, sent_to_all(): return lax.all_to_all(copies, axis, split_axis=0, concat_axis=0, tiled=True)  21.5 us
    all_gather x1, blocking collectives, on_device(): row_router = lax.all_gather(part_router, 'rows', axis=0, tiled=True)  18 us
    unnamed x9, local copies, waits for them, and re-layouts  15.3 us
    all_to_all x1, local copies, waits for them, and re-layouts, on_device(): lax.all_to_all(jnp.stack([narrow_down] * lax.axis_size('rows')), 'rows',...  15.2 us
    all_to_all x2, waiting for transfers between devices, sent_to_all(): return lax.all_to_all(copies, axis, split_axis=0, concat_axis=0, tiled=True)  11.1 us
    all_to_all x1, starting transfers between devices, on_device(): lax.all_to_all(jnp.stack([narrow_down] * lax.axis_size('rows')), 'rows',...  8.33 us
  transfers between devices with their start and end apart: 3, of which 2 were waited for; matrix products, arithmetic and copies ran while one was open for 0% of the time, Pallas kernels for 0%

profile of v1, /device:TPU:1, one launch (start us, length us, event | category | flops | bytes accessed | tf_op | source)
XLA Modules:
  0.0 351.9 jit_solution(5558363321905403555)
XLA Ops:
  0.6 0.0 copy-start
  0.6 0.0 copy-start.2
  0.7 0.0 copy-start.3
  0.7 1.9 abs_reduce_fusion
  2.6 0.7 broadcast_in_dim.8
  3.3 11.8 %all-to-all-start = ((f32[16,2,1408]{2,1,0:T(2,128)}), f32[16,2,1408]{2,1,0:T(2,128)S(1)}, u32[]{:S(2)}, u32[]{:S(2)}) async-start(f32[16,2,1408]{2,1,0:T(2,128)} %broadcast_in_dim.8), calls=%async_computation | async-start | bytes 360448 | tf_op jit(solution)/shard_map/all_to_all | solution.py:9
  15.1 0.0 copy-done.2
  15.1 0.0 copy-done.3
  15.2 18.0 %all_gather.3 = bf16[2048,2]{0,1:T(2,128)(2,1)S(1)} all-gather(bf16[128,2]{0,1:T(2,128)(2,1)S(1)} %multiply_convert_fusion), channel_id=1, replica_groups=mesh['owner'=32,'rows'=16] {'rows'}, dimensions={0}, use_global_device_ids=true | all-gather | bytes 8704 | tf_op jit(solution)/shard_map/all_gather | solution.py:34
  33.2 0.0 all-to-all-done
  33.2 0.8 broadcast_in_dim.9
  34.0 9.7 %all-to-all-start.2 = ((bf16[32,2048,2]{1,2,0:T(2,128)(2,1)}), bf16[32,2048,2]{1,2,0:T(2,128)(2,1)S(1)}, u32[]{:S(2)}, u32[]{:S(2)}) async-start(bf16[32,2048,2]{1,2,0:T(2,128)(2,1)} %broadcast_in_dim.9), calls=%async_computation.2 | async-start | bytes 524288 | tf_op jit(solution)/shard_map/all_to_all | solution.py:9
  43.7 0.1 reduce_max.19
  43.8 0.0 copy-done
  43.8 0.0 copy-start.1
  43.8 0.4 divide_convert_fusion
  44.2 11.1 %all-to-all-done.2 = bf16[32,2048,2]{1,2,0:T(2,128)(2,1)S(1)} async-done(((bf16[32,2048,2]{1,2,0:T(2,128)(2,1)}), bf16[32,2048,2]{1,2,0:T(2,128)(2,1)S(1)}, u32[]{:S(2)}, u32[]{:S(2)}) %all-to-all-start.2) | async-done | bytes 262176 | tf_op jit(solution)/shard_map/all_to_all | solution.py:9
  55.3 7.0 %stack.2 = bf16[16,2,1408,128]{3,2,1,0:T(8,128)(2,1)} broadcast(bf16[2,1408,128]{2,1,0:T(8,128)(2,1)S(1)} %divide_convert_fusion), dimensions={1,2,3} | broadcast | bytes 12255232 | tf_op jit(solution)/shard_map/stack | solution.py:31
  62.4 0.0 copy-done.1
  62.4 8.3 %all-to-all-start.1 = ((bf16[16,2,1408,128]{3,2,1,0:T(8,128)(2,1)}), bf16[16,2,1408,128]{3,2,1,0:T(8,128)(2,1)}, u32[]{:S(2)}, u32[]{:S(2)}) async-start(bf16[16,2,1408,128]{3,2,1,0:T(8,128)(2,1)} %stack.2), calls=%async_computation.1 | async-start | bytes 23068672 | tf_op jit(solution)/shard_map/all_to_all | solution.py:31
  70.7 0.8 reshape.21
  71.5 250.0 %all-to-all-done.1 = bf16[16,2,1408,128]{3,2,1,0:T(8,128)(2,1)} async-done(((bf16[16,2,1408,128]{3,2,1,0:T(8,128)(2,1)}), bf16[16,2,1408,128]{3,2,1,0:T(8,128)(2,1)}, u32[]{:S(2)}, u32[]{:S(2)}) %all-to-all-start.1) | async-done | bytes 11534368 | tf_op jit(solution)/shard_map/all_to_all | solution.py:31
  321.5 15.2 %copy.11 = bf16[16,2,1408,128]{2,3,0,1:T(8,128)(2,1)} copy(bf16[16,2,1408,128]{3,2,1,0:T(8,128)(2,1)} %all-to-all-done.1) | data formatting | bytes 23068672 | tf_op jit(solution)/shard_map/all_to_all | solution.py:31
  336.7 15.2 %copy.12 = bf16[2,1408,2048]{2,1,0:T(8,128)(2,1)} copy(bf16[2,1408,2048]{1,2,0:T(8,128)(2,1)} %bitcast.6) | data formatting | bytes 23068672
  (1 shorter events, 0.0 us)
Async XLA Ops:
  0.6 43.1 %copy-start = (f32[2,1408,128]{2,1,0:T(8,128)S(1)}, f32[2,1408,128]{2,1,0:T(8,128)}, u32[]{:S(2)}) copy-start(f32[2,1408,128]{2,1,0:T(8,128)} %param.3) | copy-start | bytes 4325380
  0.6 14.5 %copy-start.2 = (f32[128,2]{0,1:T(2,128)S(1)}, f32[128,2]{0,1:T(2,128)}, u32[]{:S(2)}) copy-start(f32[128,2]{0,1:T(2,128)} %param.4) | copy-start | bytes 3076
  0.7 14.5 %copy-start.3 = (f32[128]{0:T(128)S(1)}, f32[128]{0:T(128)}, u32[]{:S(2)}) copy-start(f32[128]{0:T(128)} %param.5) | copy-start | bytes 1540
  3.3 29.9 %all-to-all-start = ((f32[16,2,1408]{2,1,0:T(2,128)}), f32[16,2,1408]{2,1,0:T(2,128)S(1)}, u32[]{:S(2)}, u32[]{:S(2)}) async-start(f32[16,2,1408]{2,1,0:T(2,128)} %broadcast_in_dim.8), calls=%async_computation | async-start | bytes 360448 | tf_op jit(solution)/shard_map/all_to_all | solution.py:9
  34.0 21.3 %all-to-all-start.2 = ((bf16[32,2048,2]{1,2,0:T(2,128)(2,1)}), bf16[32,2048,2]{1,2,0:T(2,128)(2,1)S(1)}, u32[]{:S(2)}, u32[]{:S(2)}) async-start(bf16[32,2048,2]{1,2,0:T(2,128)(2,1)} %broadcast_in_dim.9), calls=%async_computation.2 | async-start | bytes 524288 | tf_op jit(solution)/shard_map/all_to_all | solution.py:9
  43.8 18.6 %copy-start.1 = (f32[2,1408]{1,0:T(2,128)}, f32[2,1408]{1,0:T(2,128)S(1)}, u32[]{:S(2)}) copy-start(f32[2,1408]{1,0:T(2,128)S(1)} %reduce_max.19) | copy-start | bytes 33796
  62.4 259.1 %all-to-all-start.1 = ((bf16[16,2,1408,128]{3,2,1,0:T(8,128)(2,1)}), bf16[16,2,1408,128]{3,2,1,0:T(8,128)(2,1)}, u32[]{:S(2)}, u32[]{:S(2)}) async-start(bf16[16,2,1408,128]{3,2,1,0:T(8,128)(2,1)} %stack.2), calls=%async_computation.1 | async-start | bytes 23068672 | tf_op jit(solution)/shard_map/all_to_all | solution.py:31
